TPU v7x, 256 devices: a whole 4x4x8 slice. The times are simulated.
256 devices in a mesh: section: 8 (over x, core), ep: 32 (over y, z).
Axes of the slice: x: 4, y: 4, z: 8, core: 2. Of those that a mesh axis runs over, the one named last changes fastest.
Arguments:
- hidden_states: bfloat16 [1536, 6144], P('ep'), may hold values from -6 to 6
- route_experts: int32 [1536, 2], P('ep'), may hold values from 0 to 7, all different within a row; in each aligned block of 48 rows (0 to 47, 48 to 95, ...) at most 24 rows name the same one
- route_weights: float32 [1536, 2], P('ep'), may hold values from 0.05 to 1
- gate_weight: bfloat16 [32, 6144, 2048], P('ep', None, 'section'), may hold values from -0.078125 to 0.078125
- up_weight: bfloat16 [32, 6144, 2048], P('ep', None, 'section'), may hold values from -0.078125 to 0.078125
- down_weight: bfloat16 [32, 2048, 6144], P('ep', 'section'), may hold values from -0.0625 to 0.0625
Outputs:
- layer_out: bfloat16 [1536, 6144], P('ep', 'section')
Inputs may be any that keep to these rules, and one draw needn't show every extreme that they name: `route_experts`: each row names two different experts. Among the 48 rows of one ep index no expert is named by more than 24 rows, and in every draw some expert is named by exactly 24 rows of some ep index.
All inputs are finite; a program needn't handle non-finite values.
Results may differ from a plain program's by a relative error of at most 0.015.
Values may be sent and summed in bfloat16 or wider, within the bound.
A program may use at most 128 MiB of HBM per device.

v0:
```python
import jax
import jax.numpy as jnp
from jax import lax
from jax.sharding import PartitionSpec as P

EXPERTS = 8


def cut_along(x, dim, peers):
    before, after = (x.shape[:dim], x.shape[dim + 1 :])
    return jnp.moveaxis(x.reshape(*before, peers, -1, *after), dim, 0)


def sent_and_summed(x, axis, dim):
    peers = lax.axis_size(axis)
    parts = lax.all_to_all(cut_along(x, dim, peers), axis, 0, 0, tiled=True)
    return jnp.sum(parts.astype(jnp.float32), axis=0)


def expert_rows(incoming, gate_weight, up_weight, down_weight):
    sources, slot_count, features = incoming.shape
    stacked = incoming.reshape(sources * slot_count, features)
    gate_value = jnp.dot(stacked, gate_weight[0], preferred_element_type=jnp.float32)
    up_value = jnp.dot(stacked, up_weight[0], preferred_element_type=jnp.float32)
    hidden = (jax.nn.silu(gate_value) * up_value).astype(jnp.bfloat16)
    result = jnp.dot(hidden, down_weight[0], preferred_element_type=jnp.float32).astype(
        jnp.bfloat16
    )
    return result.reshape(sources, slot_count, features)


def on_device(hidden_states, route_experts, route_weights, gate_weight, up_weight, down_weight):
    ep_count = lax.axis_size("ep")
    section_count = lax.axis_size("section")
    tok_rows, features = hidden_states.shape
    members = ep_count // EXPERTS
    capacity = tok_rows // 2
    chosen = route_experts.reshape(-1)
    one_hot = (chosen[:, None] == jnp.arange(EXPERTS, dtype=jnp.int32)[None, :]).astype(jnp.int32)
    earlier = jnp.cumsum(one_hot, axis=0) - one_hot
    slot_index = jnp.sum(earlier * one_hot, axis=1)
    position = (chosen * capacity + slot_index).reshape(tok_rows, 2)
    columns = jnp.arange(EXPERTS * capacity, dtype=jnp.int32)
    matches = position[:, :, None] == columns[None, None, :]
    select = jnp.sum(matches.astype(jnp.int32), axis=1).astype(jnp.bfloat16)
    weighing = jnp.sum(matches.astype(jnp.float32) * route_weights[:, :, None], axis=1)
    packed = jnp.einsum(
        "tj,td->jd", select, hidden_states, preferred_element_type=jnp.float32
    ).astype(jnp.bfloat16)
    outgoing = jnp.repeat(packed.reshape(EXPERTS, capacity, features), members, axis=0)
    slot_share = capacity // section_count
    first_slot = lax.axis_index("section") * slot_share
    own_slots = lax.dynamic_slice_in_dim(outgoing, first_slot, slot_share, 1)
    arrived = lax.all_to_all(own_slots, "ep", split_axis=0, concat_axis=0, tiled=True)
    partials = expert_rows(
        lax.all_gather(arrived, "section", axis=1, tiled=True), gate_weight, up_weight, down_weight
    )
    summed = lax.psum_scatter(
        partials.astype(jnp.float32).astype(jnp.bfloat16),
        "section",
        scatter_dimension=1,
        tiled=True,
    ).astype(jnp.float32)
    returned = lax.all_to_all(
        summed.astype(jnp.bfloat16), "ep", split_axis=0, concat_axis=0, tiled=True
    ).astype(summed.dtype)
    merged = jnp.sum(returned.reshape(EXPERTS, members, slot_share, features), axis=1)
    weigh_part = lax.dynamic_slice_in_dim(
        weighing.reshape(tok_rows, EXPERTS, capacity), first_slot, slot_share, 2
    )
    contribution = jnp.dot(
        weigh_part.reshape(tok_rows, EXPERTS * slot_share),
        merged.reshape(EXPERTS * slot_share, features),
        preferred_element_type=jnp.float32,
    )
    layer_out = sent_and_summed(contribution.astype(jnp.bfloat16), "section", 1)
    return layer_out.astype(jnp.bfloat16)


def solution(mesh):
    return jax.shard_map(
        on_device,
        mesh=mesh,
        in_specs=(
            P("ep", None),
            P("ep", None),
            P("ep", None),
            P("ep", None, "section"),
            P("ep", None, "section"),
            P("ep", "section", None),
        ),
        out_specs=P("ep", "section"),
        check_vma=False,
    )
```

profile of v0, /device:TPU:1, one launch (start us, length us, event | category | flops | bytes accessed | tf_op | source)
XLA Modules:
  0.0 317.6 jit_solution(11855568616730549436)
XLA Ops:
  6.5 0.9 copy.60
  7.5 0.1 eq.28
  7.6 0.1 fusion.21
  7.7 0.1 reduce_window_sum.11
  7.8 0.2 select_reduce_fusion.1
  8.0 0.1 reduce_sum.51
  8.1 0.1 copy.61
  8.2 0.7 multiply_add_fusion
  8.9 0.1 convert_reduce_fusion.1
  9.0 1.9 convolution_convert_fusion.1
  10.8 4.8 %broadcast_in_dim.2 = bf16[8,4,24,6144]{3,2,1,0:T(8,128)(2,1)} broadcast(bf16[8,24,6144]{2,1,0:T(8,128)(2,1)S(1)} %bitcast.41), dimensions={0,2,3} | broadcast | bytes 11796480 | tf_op jit(solution)/shard_map/broadcast_in_dim | solution.py:50
  15.6 4.0 %constant_dynamic-slice_fusion.1 = bf16[32,3,6144]{2,1,0:T(4,128)(2,1)S(1)} fusion(bf16[32,24,6144]{2,1,0:T(8,128)(2,1)} %bitcast.37, s32[]{:T(128)S(6)} %select_n.4), kind=kLoop, calls=%fused_computation.30 | loop fusion | bytes 2359300 | tf_op jit(solution)/shard_map/dynamic_slice | solution.py:53
  19.6 48.3 %all_to_all.15 = bf16[32,3,6144]{2,1,0:T(4,128)(2,1)S(1)} all-to-all(bf16[32,3,6144]{2,1,0:T(4,128)(2,1)S(1)} %constant_dynamic-slice_fusion.1), channel_id=1, replica_groups=mesh['section'=8,'ep'=32] {'ep'}, dimensions={0} | all-to-all | bytes 2359296 | tf_op jit(solution)/shard_map/all_to_all | solution.py:54
  67.9 1.9 copy.64
  69.8 0.0 all-gather.2.cloned.1.call-update
  69.8 0.2 reduce-scatter.2.cloned.1.call-start
  70.0 57.2 %all-gather.2.cloned.1.call-done = bf16[32,24,6144]{2,0,1:T(8,128)(2,1)} async-done(((bf16[32,3,6144]{2,0,1:T(8,128)(2,1)}), bf16[32,24,6144]{2,0,1:T(8,128)(2,1)}) %all-gather.2.cloned.1.call-update) | async-done | bytes 9437200 | tf_op jit(solution)/shard_map/all_gather | solution.py:56
  127.2 12.5 %copy.65 = bf16[32,24,6144]{2,1,0:T(8,128)(2,1)} copy(bf16[32,24,6144]{2,0,1:T(8,128)(2,1)} %all-gather.2.cloned.1.call-done) | data formatting | bytes 18874368 | tf_op jit(solution)/shard_map/all_gather | solution.py:56
  139.7 8.1 %fusion.4 = f32[768,256]{1,0:T(8,128)} fusion(bf16[768,6144]{1,0:T(8,128)(2,1)} %bitcast.38, bf16[1,6144,256]{2,1,0:T(8,128)(2,1)} %param.9), kind=kOutput, calls=%fused_computation.8 | convolution fusion | flops 2415919104 | bytes 13369344 | tf_op jit(solution)/shard_map/dot_general | solution.py:23
  147.7 19.4 %convolution_convert_fusion = bf16[768,6144]{1,0:T(8,128)(2,1)} fusion(bf16[1,256,6144]{2,1,0:T(8,128)(2,1)S(1)} %copy-done, bf16[768,6144]{1,0:T(8,128)(2,1)} %bitcast.39, bf16[1,6144,256]{2,1,0:T(8,128)(2,1)} %param.10, f32[768,256]{1,0:T(8,128)} %fusion.4), kind=kOutput, calls=%fused_computation | convolution fusion | flops 4837736448 | bytes 25952256 | tf_op jit(solution)/shard_map/dot_general | solution.py:26
  167.1 12.5 %copy.66 = bf16[32,24,6144]{2,0,1:T(8,128)(2,1)} copy(bf16[32,24,6144]{2,1,0:T(8,128)(2,1)} %bitcast.40) | data formatting | bytes 18874368 | tf_op jit(solution)/shard_map/reshape | solution.py:29
  179.6 0.0 reduce-scatter.2.cloned.1.call-update
  179.7 59.5 %reduce-scatter.2.cloned.1.call-done = bf16[32,3,6144]{2,0,1:T(8,128)(2,1)} async-done(((bf16[32,24,6144]{2,0,1:T(8,128)(2,1)}), bf16[32,3,6144]{2,0,1:T(8,128)(2,1)}) %reduce-scatter.2.cloned.1.call-update) | async-done | bytes 1179664 | tf_op jit(solution)/shard_map/reduce_scatter | solution.py:58
  239.1 3.4 %copy.67 = bf16[32,3,6144]{2,1,0:T(4,128)(2,1)} copy(bf16[32,3,6144]{2,0,1:T(8,128)(2,1)} %reduce-scatter.2.cloned.1.call-done) | data formatting | bytes 2359296 | tf_op jit(solution)/shard_map/reduce_scatter | solution.py:58
  242.5 9.7 %all-to-all-start.1 = ((bf16[32,3,6144]{2,1,0:T(4,128)(2,1)}), bf16[32,3,6144]{2,1,0:T(4,128)(2,1)}, u32[]{:S(2)}, u32[]{:S(2)}) async-start(bf16[32,3,6144]{2,1,0:T(4,128)(2,1)} %copy.67), calls=%async_computation.2 | async-start | bytes 3145728 | tf_op jit(solution)/shard_map/all_to_all | solution.py:64
  252.3 0.1 select_reduce_fusion
  252.4 0.1 copy.62
  252.5 36.7 %all-to-all-done.1 = bf16[32,3,6144]{2,1,0:T(4,128)(2,1)} async-done(((bf16[32,3,6144]{2,1,0:T(4,128)(2,1)}), bf16[32,3,6144]{2,1,0:T(4,128)(2,1)}, u32[]{:S(2)}, u32[]{:S(2)}) %all-to-all-start.1) | async-done | bytes 1179680 | tf_op jit(solution)/shard_map/all_to_all | solution.py:64
  289.2 2.4 convert_reduce_fusion
  291.5 0.4 fusion
  292.0 17.0 %all_to_all.16 = bf16[8,48,768]{2,1,0:T(8,128)(2,1)} all-to-all(bf16[8,48,768]{2,1,0:T(8,128)(2,1)S(1)} %bitcast.43), channel_id=1, replica_groups=mesh['section'=8,'ep'=32] {'section'}, dimensions={0} | all-to-all | bytes 1179648 | tf_op jit(solution)/shard_map/all_to_all | solution.py:16
  308.9 1.8 reduce_sum.55
  (9 shorter events, 0.1 us)
Async XLA Ops:
  6.5 141.2 %copy-start = (bf16[1,256,6144]{2,1,0:T(8,128)(2,1)S(1)}, bf16[1,256,6144]{2,1,0:T(8,128)(2,1)}, u32[]{:S(2)}) copy-start(bf16[1,256,6144]{2,1,0:T(8,128)(2,1)} %param.11) | copy-start | bytes 9437188
  6.5 120.6 %all-gather.2.cloned.1.call-start = ((), (), s32[]{:S(2)}) async-start(), calls=%async_computation.4 | async-start | bytes 10616832 | tf_op jit(solution)/shard_map/all_gather | solution.py:56
  69.8 169.3 %reduce-scatter.2.cloned.1.call-start = ((), (), s32[]{:S(2)}) async-start(), calls=%async_computation.5 | async-start | bytes 10616832 | tf_op jit(solution)/shard_map/reduce_scatter | solution.py:58
  179.6 72.6 %copy-start.2 = (f32[48,2]{0,1:T(2,128)S(1)}, f32[48,2]{0,1:T(2,128)}, u32[]{:S(2)}) copy-start(f32[48,2]{0,1:T(2,128)} %param.8) | copy-start | bytes 1156
  242.5 46.6 %all-to-all-start.1 = ((bf16[32,3,6144]{2,1,0:T(4,128)(2,1)}), bf16[32,3,6144]{2,1,0:T(4,128)(2,1)}, u32[]{:S(2)}, u32[]{:S(2)}) async-start(bf16[32,3,6144]{2,1,0:T(4,128)(2,1)} %copy.67), calls=%async_computation.2 | async-start | bytes 3145728 | tf_op jit(solution)/shard_map/all_to_all | solution.py:64
  252.2 58.5 %copy-start.1 = (bf16[1,256,6144]{2,1,0:T(8,128)(2,1)S(1)}, bf16[1,256,6144]{2,1,0:T(8,128)(2,1)}, u32[]{:S(2)}) copy-start(bf16[1,256,6144]{2,1,0:T(8,128)(2,1)} %param.11) | copy-start | bytes 9437188
Sparse Core Ops, SparseCore 0:
  69.9 57.2 all-gather.1
  179.8 59.3 reduce-scatter.1
where the time goes:
time: 318 us
  waiting for transfers between devices  153 us (48%)
  blocking collectives  65.3 us (21%)
  local copies, waits for them, and re-layouts  40.4 us (13%)
  matrix products  29.7 us (9%)
  between operations  13.5 us (4%)
  starting transfers between devices  9.91 us (3%)
  other arithmetic  5.43 us (2%)
    reduce_scatter x1, waiting for transfers between devices, on_device(): lax.psum_scatter(partials.astype(jnp.float32).astype(jnp.bfloat16), 'sect...  59.5 us
    all_gather x1, waiting for transfers between devices, on_device(): lax.all_gather(arrived, 'section', axis=1, tiled=True)  57.2 us
    all_to_all x1, blocking collectives, on_device(): lax.all_to_all(own_slots, 'ep', split_axis=0, concat_axis=0, tiled=True)  48.3 us
    all_to_all x1, waiting for transfers between devices, on_device(): lax.all_to_all(summed.astype(jnp.bfloat16), 'ep', split_axis=0, concat_ax...  36.7 us
    dot_general x1, matrix products, expert_rows(): jnp.dot(hidden, down_weight[0], preferred_element_type=jnp.float32)  19.4 us
    all_to_all x1, blocking collectives, sent_and_summed(): parts = lax.all_to_all(cut_along(x, dim, peers), axis, 0, 0, tiled=True)  17 us
    reshape x1, local copies, waits for them, and re-layouts, expert_rows(): return result.reshape(sources, slot_count, features)  12.5 us
    all_gather x1, local copies, waits for them, and re-layouts, on_device(): lax.all_gather(arrived, 'section', axis=1, tiled=True)  12.5 us
  transfers between devices with their start and end apart: 3, of which 3 were waited for; matrix products, arithmetic and copies ran while one was open for 0% of the time, Pallas kernels for 0%

commit v1 on v0

--- a/solution.py
+++ b/solution.py
@@ -30,6 +30,32 @@
 
 
 def on_device(hidden_states, route_experts, route_weights, gate_weight, up_weight, down_weight):
+
+    def expand_cubes_over_axis(packet, dim_k, axis_key="section"):
+        step_out, local_out, item_now = (
+            lax.axis_size(axis_key),
+            lax.axis_index(axis_key),
+            packet.shape[dim_k],
+        )
+        found = [dev * step_out if t == dim_k else dev for t, dev in enumerate(packet.shape)]
+        val = lax.dynamic_update_slice_in_dim(
+            jnp.zeros(found, packet.dtype), packet, local_out * item_now, axis=dim_k
+        )
+        y = mat_out = packet
+        for dd in range(1, step_out // 2 + 1):
+            y = lax.ppermute(y, axis_key, [(t, (t + 1) % step_out) for t in range(step_out)])
+            val = lax.dynamic_update_slice_in_dim(
+                val, y, (local_out - dd) % step_out * item_now, axis=dim_k
+            )
+            if 2 * dd < step_out:
+                mat_out = lax.ppermute(
+                    mat_out, axis_key, [(t, (t - 1) % step_out) for t in range(step_out)]
+                )
+                val = lax.dynamic_update_slice_in_dim(
+                    val, mat_out, (local_out + dd) % step_out * item_now, axis=dim_k
+                )
+        return val
+
     ep_count = lax.axis_size("ep")
     section_count = lax.axis_size("section")
     tok_rows, features = hidden_states.shape
@@ -52,9 +78,7 @@
     first_slot = lax.axis_index("section") * slot_share
     own_slots = lax.dynamic_slice_in_dim(outgoing, first_slot, slot_share, 1)
     arrived = lax.all_to_all(own_slots, "ep", split_axis=0, concat_axis=0, tiled=True)
-    partials = expert_rows(
-        lax.all_gather(arrived, "section", axis=1, tiled=True), gate_weight, up_weight, down_weight
-    )
+    partials = expert_rows(expand_cubes_over_axis(arrived, 1), gate_weight, up_weight, down_weight)
     summed = lax.psum_scatter(
         partials.astype(jnp.float32).astype(jnp.bfloat16),
         "section",

time: 318 us -> 503 us (1.58)
  local copies, waits for them, and re-layouts: 40.4 us -> 228 us
  waiting for transfers between devices: 153 us -> 132 us
  starting transfers between devices: 9.91 us -> 23.4 us
    dynamic_update_slice x0 -> x8, local copies, waits for them, and re-layouts: none -> 170 us  [the longest x4 84.2 us: expand_cubes_over_axis(): lax.dynamic_update_slice_in_dim(val, y, (local_out - dd) % step_out * ite...]
    all_gather x1 -> x0, waiting for transfers between devices: 57.2 us -> none  [on_device(): lax.all_gather(arrived, 'section', axis=1, tiled=True)]
    ppermute x0 -> x7, waiting for transfers between devices: none -> 37 us  [the longest x4 35.9 us: expand_cubes_over_axis(): lax.ppermute(y, axis_key, [(t, (t + 1) % step_out) for t in range(step_ou...]
    ppermute x0 -> x7, local copies, waits for them, and re-layouts: none -> 24.1 us  [the longest x4 13.8 us: expand_cubes_over_axis(): lax.ppermute(y, axis_key, [(t, (t + 1) % step_out) for t in range(step_ou...]
    ppermute x0 -> x7, starting transfers between devices: none -> 13.7 us  [the longest x4 12.4 us: expand_cubes_over_axis(): lax.ppermute(y, axis_key, [(t, (t + 1) % step_out) for t in range(step_ou...]
    all_gather x1 -> x0, local copies, waits for them, and re-layouts: 12.5 us -> none  [on_device(): lax.all_gather(arrived, 'section', axis=1, tiled=True)]
  transfers between devices with their start and end apart: 3 -> 9, of which waited for: 3 -> 6; matrix products, arithmetic and copies ran while one was open for 0% -> 35% of each run, Pallas kernels for 0% -> 0%
where the time goes in v1:
time: 503 us; the launch traced here: 498 us
  local copies, waits for them, and re-layouts  228 us (45%)
  waiting for transfers between devices  132 us (26%)
  blocking collectives  65.3 us (13%)
  matrix products  29.7 us (6%)
  starting transfers between devices  23.4 us (5%)
  between operations  13.5 us (3%)
  other arithmetic  5.43 us (1%)
    dynamic_update_slice x4, local copies, waits for them, and re-layouts, expand_cubes_over_axis(): lax.dynamic_update_slice_in_dim(val, y, (local_out - dd) % step_out * ite...  84.2 us
    dynamic_update_slice x3, local copies, waits for them, and re-layouts, expand_cubes_over_axis(): lax.dynamic_update_slice_in_dim(val, mat_out, (local_out + dd) % step_out...  64.5 us
    reduce_scatter x1, waiting for transfers between devices, on_device(): lax.psum_scatter(partials.astype(jnp.float32).astype(jnp.bfloat16), 'sect...  58.6 us
    all_to_all x1, blocking collectives, on_device(): lax.all_to_all(own_slots, 'ep', split_axis=0, concat_axis=0, tiled=True)  48.3 us
    all_to_all x1, waiting for transfers between devices, on_device(): lax.all_to_all(summed.astype(jnp.bfloat16), 'ep', split_axis=0, concat_ax...  36.7 us
    ppermute x4, waiting for transfers between devices, expand_cubes_over_axis(): lax.ppermute(y, axis_key, [(t, (t + 1) % step_out) for t in range(step_ou...  35.9 us
    dynamic_update_slice x1, local copies, waits for them, and re-layouts, expand_cubes_over_axis(): lax.dynamic_update_slice_in_dim(jnp.zeros(found, packet.dtype), packet, l...  21.5 us
    dot_general x1, matrix products, expert_rows(): jnp.dot(hidden, down_weight[0], preferred_element_type=jnp.float32)  19.4 us
  transfers between devices with their start and end apart: 9, of which 6 were waited for; matrix products, arithmetic and copies ran while one was open for 35% of the time, Pallas kernels for 0%

profile of v1, /device:TPU:1, one launch (start us, length us, event | category | flops | bytes accessed | tf_op | source)
XLA Modules:
  0.0 498.0 jit_solution(6945314227604992000)
XLA Ops:
  10.8 4.8 broadcast_in_dim.10
  15.6 4.0 constant_dynamic-slice_fusion
  19.6 48.3 %all_to_all.15 = bf16[32,3,6144]{2,1,0:T(4,128)(2,1)S(1)} all-to-all(bf16[32,3,6144]{2,1,0:T(4,128)(2,1)S(1)} %constant_dynamic-slice_fusion), channel_id=1, replica_groups=mesh['section'=8,'ep'=32] {'ep'}, dimensions={0} | all-to-all | bytes 2359296 | tf_op jit(solution)/shard_map/all_to_all | solution.py:80
  69.9 4.8 collective-permute-start
  74.8 13.1 %collective-permute-done = bf16[32,3,6144]{2,0,1:T(8,128)(2,1)S(1)} collective-permute-done((bf16[32,3,6144]{2,0,1:T(8,128)(2,1)S(1)}, bf16[32,3,6144]{2,0,1:T(8,128)(2,1)S(1)}, u32[]{:S(2)}, u32[]{:S(2)}) %collective-permute-start) | collective-permute-done | bytes 1179680 | tf_op jit(solution)/shard_map/ppermute | solution.py:46
  91.6 11.9 %collective-permute-done.2 = bf16[32,3,6144]{2,0,1:T(8,128)(2,1)S(1)} collective-permute-done((bf16[32,3,6144]{2,0,1:T(8,128)(2,1)S(1)}, bf16[32,3,6144]{2,0,1:T(8,128)(2,1)S(1)}, u32[]{:S(2)}, u32[]{:S(2)}) %collective-permute-start.2) | collective-permute-done | bytes 1179680 | tf_op jit(solution)/shard_map/ppermute | solution.py:46
  108.4 10.8 %collective-permute-done.4 = bf16[32,3,6144]{2,0,1:T(8,128)(2,1)} collective-permute-done((bf16[32,3,6144]{2,0,1:T(8,128)(2,1)S(1)}, bf16[32,3,6144]{2,0,1:T(8,128)(2,1)}, u32[]{:S(2)}, u32[]{:S(2)}) %collective-permute-start.4) | collective-permute-done | bytes 1179680 | tf_op jit(solution)/shard_map/ppermute | solution.py:46
  119.2 2.6 collective-permute-start.6
  121.8 4.8 broadcast_in_dim.4
  126.6 21.5 %dynamic_update_slice.24 = bf16[32,24,6144]{2,1,0:T(8,128)(2,1)} dynamic-update-slice(bf16[32,24,6144]{2,1,0:T(8,128)(2,1)} %broadcast_in_dim.4, bf16[32,3,6144]{2,1,0:T(4,128)(2,1)} %copy-done.1, s32[]{:T(128)} %constant.60.clone.1, s32[]{:T(128)S(6)} %select_n.57, s32[]{:T(128)} %constant.60.clone.1) | dynamic-update-slice | bytes 2359300 | tf_op jit(solution)/shard_map/dynamic_update_slice | solution.py:41
  148.1 3.5 copy.86
  151.5 21.5 %dynamic_update_slice.25 = bf16[32,24,6144]{2,1,0:T(8,128)(2,1)} dynamic-update-slice(bf16[32,24,6144]{2,1,0:T(8,128)(2,1)} %dynamic_update_slice.24, bf16[32,3,6144]{2,1,0:T(4,128)(2,1)} %copy.86, s32[]{:T(128)} %constant.60.clone.1, s32[]{:T(128)S(6)} %select_n.59, s32[]{:T(128)} %constant.60.clone.1) | dynamic-update-slice | bytes 2359300 | tf_op jit(solution)/shard_map/dynamic_update_slice | solution.py:47
  173.1 3.4 copy.88
  176.5 21.5 %dynamic_update_slice.26 = bf16[32,24,6144]{2,1,0:T(8,128)(2,1)} dynamic-update-slice(bf16[32,24,6144]{2,1,0:T(8,128)(2,1)} %dynamic_update_slice.25, bf16[32,3,6144]{2,1,0:T(4,128)(2,1)} %copy.88, s32[]{:T(128)} %constant.60.clone.1, s32[]{:T(128)S(6)} %select_n.61, s32[]{:T(128)} %constant.60.clone.1) | dynamic-update-slice | bytes 2359300 | tf_op jit(solution)/shard_map/dynamic_update_slice | solution.py:54
  198.0 3.4 copy.89
  201.4 20.6 %dynamic_update_slice.27 = bf16[32,24,6144]{2,1,0:T(8,128)(2,1)} dynamic-update-slice(bf16[32,24,6144]{2,1,0:T(8,128)(2,1)} %dynamic_update_slice.26, bf16[32,3,6144]{2,1,0:T(4,128)(2,1)} %copy.89, s32[]{:T(128)} %constant.60.clone.1, s32[]{:T(128)S(6)} %select_n.63, s32[]{:T(128)} %constant.60.clone.1) | dynamic-update-slice | bytes 2359300 | tf_op jit(solution)/shard_map/dynamic_update_slice | solution.py:47
  222.0 3.4 copy.90
  225.4 21.5 %dynamic_update_slice.28 = bf16[32,24,6144]{2,1,0:T(8,128)(2,1)} dynamic-update-slice(bf16[32,24,6144]{2,1,0:T(8,128)(2,1)} %dynamic_update_slice.27, bf16[32,3,6144]{2,1,0:T(4,128)(2,1)} %copy.90, s32[]{:T(128)} %constant.60.clone.1, s32[]{:T(128)S(6)} %select_n.65, s32[]{:T(128)} %constant.60.clone.1) | dynamic-update-slice | bytes 2359300 | tf_op jit(solution)/shard_map/dynamic_update_slice | solution.py:54
  247.0 3.4 copy.91
  250.4 20.6 %dynamic_update_slice.29 = bf16[32,24,6144]{2,1,0:T(8,128)(2,1)} dynamic-update-slice(bf16[32,24,6144]{2,1,0:T(8,128)(2,1)} %dynamic_update_slice.28, bf16[32,3,6144]{2,1,0:T(4,128)(2,1)} %copy.91, s32[]{:T(128)} %constant.60.clone.1, s32[]{:T(128)S(6)} %select_n.67, s32[]{:T(128)} %constant.60.clone.1) | dynamic-update-slice | bytes 2359300 | tf_op jit(solution)/shard_map/dynamic_update_slice | solution.py:47
  271.0 3.4 copy.92
  274.4 21.5 %dynamic_update_slice.30 = bf16[32,24,6144]{2,1,0:T(8,128)(2,1)} dynamic-update-slice(bf16[32,24,6144]{2,1,0:T(8,128)(2,1)} %dynamic_update_slice.29, bf16[32,3,6144]{2,1,0:T(4,128)(2,1)} %copy.92, s32[]{:T(128)} %constant.60.clone.1, s32[]{:T(128)S(6)} %select_n.69, s32[]{:T(128)} %constant.60.clone.1) | dynamic-update-slice | bytes 2359300 | tf_op jit(solution)/shard_map/dynamic_update_slice | solution.py:54
  295.9 3.5 copy.93
  299.4 21.5 %dynamic_update_slice.31 = bf16[32,24,6144]{2,1,0:T(8,128)(2,1)} dynamic-update-slice(bf16[32,24,6144]{2,1,0:T(8,128)(2,1)} %dynamic_update_slice.30, bf16[32,3,6144]{2,1,0:T(4,128)(2,1)} %copy.93, s32[]{:T(128)} %constant.60.clone.1, s32[]{:T(128)S(6)} %select_n.71, s32[]{:T(128)} %constant.60.clone.1) | dynamic-update-slice | bytes 2359300 | tf_op jit(solution)/shard_map/dynamic_update_slice | solution.py:47
  320.9 8.1 %fusion.2 = f32[768,256]{1,0:T(8,128)} fusion(bf16[768,6144]{1,0:T(8,128)(2,1)} %bitcast.37, bf16[1,6144,256]{2,1,0:T(8,128)(2,1)} %param.10), kind=kOutput, calls=%fused_computation.6 | convolution fusion | flops 2415919104 | bytes 13369344 | tf_op jit(solution)/shard_map/dot_general | solution.py:24
  329.0 19.4 %convolution_convert_fusion = bf16[768,6144]{1,0:T(8,128)(2,1)} fusion(bf16[1,256,6144]{2,1,0:T(8,128)(2,1)S(1)} %copy-done, f32[768,256]{1,0:T(8,128)} %fusion.2, bf16[768,6144]{1,0:T(8,128)(2,1)} %bitcast.38, bf16[1,6144,256]{2,1,0:T(8,128)(2,1)} %param.9), kind=kOutput, calls=%fused_computation | convolution fusion | flops 4837736448 | bytes 25952256 | tf_op jit(solution)/shard_map/dot_general | solution.py:26
  348.4 12.5 %copy.94 = bf16[32,24,6144]{2,0,1:T(8,128)(2,1)} copy(bf16[32,24,6144]{2,1,0:T(8,128)(2,1)} %bitcast.36) | data formatting | bytes 18874368 | tf_op jit(solution)/shard_map/reshape | solution.py:29
  360.9 58.6 %reduce-scatter.2.cloned.1.call-done = bf16[32,3,6144]{2,0,1:T(8,128)(2,1)} async-done(((bf16[32,24,6144]{2,0,1:T(8,128)(2,1)}), bf16[32,3,6144]{2,0,1:T(8,128)(2,1)}) %reduce-scatter.2.cloned.1.call-update) | async-done | bytes 1179664 | tf_op jit(solution)/shard_map/reduce_scatter | solution.py:82
  419.6 3.4 copy.95
  423.0 9.7 %all-to-all-start.1 = ((bf16[32,3,6144]{2,1,0:T(4,128)(2,1)}), bf16[32,3,6144]{2,1,0:T(4,128)(2,1)}, u32[]{:S(2)}, u32[]{:S(2)}) async-start(bf16[32,3,6144]{2,1,0:T(4,128)(2,1)} %copy.95), calls=%async_computation.2 | async-start | bytes 3145728 | tf_op jit(solution)/shard_map/all_to_all | solution.py:88
  432.9 36.7 %all-to-all-done.1 = bf16[32,3,6144]{2,1,0:T(4,128)(2,1)} async-done(((bf16[32,3,6144]{2,1,0:T(4,128)(2,1)}), bf16[32,3,6144]{2,1,0:T(4,128)(2,1)}, u32[]{:S(2)}, u32[]{:S(2)}) %all-to-all-start.1) | async-done | bytes 1179680 | tf_op jit(solution)/shard_map/all_to_all | solution.py:88
  472.4 17.0 %all_to_all.16 = bf16[8,48,768]{2,1,0:T(8,128)(2,1)} all-to-all(bf16[8,48,768]{2,1,0:T(8,128)(2,1)S(1)} %bitcast.41), channel_id=1, replica_groups=mesh['section'=8,'ep'=32] {'section'}, dimensions={0} | all-to-all | bytes 1179648 | tf_op jit(solution)/shard_map/all_to_all | solution.py:16
  (41 shorter events, 19.6 us)
Async XLA Ops:
  6.5 322.5 %copy-start = (bf16[1,256,6144]{2,1,0:T(8,128)(2,1)S(1)}, bf16[1,256,6144]{2,1,0:T(8,128)(2,1)}, u32[]{:S(2)}) copy-start(bf16[1,256,6144]{2,1,0:T(8,128)(2,1)} %param.11) | copy-start | bytes 9437188
  6.5 413.0 %reduce-scatter.2.cloned.1.call-start = ((), (), s32[]{:S(2)}) async-start(), calls=%async_computation.4 | async-start | bytes 10616832 | tf_op jit(solution)/shard_map/reduce_scatter | solution.py:82
  67.9 1.2 copy-start.1
  69.9 18.0 %collective-permute-start = (bf16[32,3,6144]{2,0,1:T(8,128)(2,1)S(1)}, bf16[32,3,6144]{2,0,1:T(8,128)(2,1)S(1)}, u32[]{:S(2)}, u32[]{:S(2)}) collective-permute-start(bf16[32,3,6144]{2,0,1:T(8,128)(2,1)S(1)} %copy.85), channel_id=1, source_target_pairs={{0,32},{32,64},{64,96},{96,128},{128,160},{160,192},{192,224},{224... | collective-permute-start | bytes 3538952 | tf_op jit(solution)/shard_map/ppermute | solution.py:46
  74.8 15.6 %collective-permute-start.1 = (bf16[32,3,6144]{2,0,1:T(8,128)(2,1)S(1)}, bf16[32,3,6144]{2,0,1:T(8,128)(2,1)S(1)}, u32[]{:S(2)}, u32[]{:S(2)}) collective-permute-start(bf16[32,3,6144]{2,0,1:T(8,128)(2,1)S(1)} %copy.85), channel_id=1, source_target_pairs={{0,224},{32,0},{64,32},{96,64},{128,96},{160,128},{192,160},{224,1... | collective-permute-start | bytes 3538952 | tf_op jit(solution)/shard_map/ppermute | solution.py:51
  87.9 31.3 %copy-start.4 = (bf16[32,3,6144]{2,0,1:T(8,128)(2,1)}, bf16[32,3,6144]{2,0,1:T(8,128)(2,1)S(1)}, u32[]{:S(2)}) copy-start(bf16[32,3,6144]{2,0,1:T(8,128)(2,1)S(1)} %collective-permute-done) | copy-start | bytes 3538948
  87.9 15.6 %collective-permute-start.2 = (bf16[32,3,6144]{2,0,1:T(8,128)(2,1)S(1)}, bf16[32,3,6144]{2,0,1:T(8,128)(2,1)S(1)}, u32[]{:S(2)}, u32[]{:S(2)}) collective-permute-start(bf16[32,3,6144]{2,0,1:T(8,128)(2,1)S(1)} %collective-permute-done), channel_id=1, source_target_pairs={{0,32},{32,64},{64,96},{96,128},{128,160},{160,192},{192,224},{224... | collective-permute-start | bytes 3538952 | tf_op jit(solution)/shard_map/ppermute | solution.py:46
  90.4 1.0 copy-start.2
  91.5 15.7 %collective-permute-start.3 = (bf16[32,3,6144]{2,0,1:T(8,128)(2,1)S(1)}, bf16[32,3,6144]{2,0,1:T(8,128)(2,1)}, u32[]{:S(2)}, u32[]{:S(2)}) collective-permute-start(bf16[32,3,6144]{2,0,1:T(8,128)(2,1)S(1)} %collective-permute-done.1), channel_id=1, source_target_pairs={{0,224},{32,0},{64,32},{96,64},{128,96},{160,128},{192,160},{224,1... | collective-permute-start | bytes 3538952 | tf_op jit(solution)/shard_map/ppermute | solution.py:51
  103.6 3.6 copy-start.3
  103.6 15.6 %collective-permute-start.4 = (bf16[32,3,6144]{2,0,1:T(8,128)(2,1)S(1)}, bf16[32,3,6144]{2,0,1:T(8,128)(2,1)}, u32[]{:S(2)}, u32[]{:S(2)}) collective-permute-start(bf16[32,3,6144]{2,0,1:T(8,128)(2,1)S(1)} %collective-permute-done.2), channel_id=1, source_target_pairs={{0,32},{32,64},{64,96},{96,128},{128,160},{160,192},{192,224},{224... | collective-permute-start | bytes 3538952 | tf_op jit(solution)/shard_map/ppermute | solution.py:46
  107.2 163.8 %collective-permute-start.5 = (bf16[32,3,6144]{2,0,1:T(8,128)(2,1)}, bf16[32,3,6144]{2,0,1:T(8,128)(2,1)}, u32[]{:S(2)}, u32[]{:S(2)}) collective-permute-start(bf16[32,3,6144]{2,0,1:T(8,128)(2,1)} %collective-permute-done.3), channel_id=1, source_target_pairs={{0,224},{32,0},{64,32},{96,64},{128,96},{160,128},{192,160},{224,1... | collective-permute-start | bytes 3538952 | tf_op jit(solution)/shard_map/ppermute | solution.py:51
  119.2 176.7 %collective-permute-start.6 = (bf16[32,3,6144]{2,0,1:T(8,128)(2,1)}, bf16[32,3,6144]{2,0,1:T(8,128)(2,1)}, u32[]{:S(2)}, u32[]{:S(2)}) collective-permute-start(bf16[32,3,6144]{2,0,1:T(8,128)(2,1)} %collective-permute-done.4), channel_id=1, source_target_pairs={{0,32},{32,64},{64,96},{96,128},{128,160},{160,192},{192,224},{224... | collective-permute-start | bytes 3538952 | tf_op jit(solution)/shard_map/ppermute | solution.py:46
  360.9 71.8 %copy-start.5 = (f32[48,2]{0,1:T(2,128)S(1)}, f32[48,2]{0,1:T(2,128)}, u32[]{:S(2)}) copy-start(f32[48,2]{0,1:T(2,128)} %param.8) | copy-start | bytes 1156
  423.0 46.6 %all-to-all-start.1 = ((bf16[32,3,6144]{2,1,0:T(4,128)(2,1)}), bf16[32,3,6144]{2,1,0:T(4,128)(2,1)}, u32[]{:S(2)}, u32[]{:S(2)}) async-start(bf16[32,3,6144]{2,1,0:T(4,128)(2,1)} %copy.95), calls=%async_computation.2 | async-start | bytes 3145728 | tf_op jit(solution)/shard_map/all_to_all | solution.py:88
Sparse Core Ops, SparseCore 0:
  361.0 58.4 reduce-scatter.1
